TPU v7x, 32 devices: a whole 2x2x4 slice. The times are simulated.
32 devices in a mesh: group: 1, ctx: 32 (over z, y, x, core).
Axes of the slice: x: 2, y: 2, z: 4, core: 2. Of those that a mesh axis runs over, the one named last changes fastest.
Arguments:
- queries: bfloat16 [2, 64, 128], P('group'), may hold values from -80 to 80
- key_cache: bfloat16 [2, 4096, 512], P('group', 'ctx'), may hold values from -4 to 4
- value_cache: bfloat16 [2, 4096, 512], P('group', 'ctx'), may hold values from -6 to 6
- out_weight: bfloat16 [8192, 4096], P('ctx'), may hold values from -0.125 to 0.125
- hidden_in: bfloat16 [2, 4096], P('group'), may hold values from -45 to 45
- norm_gain: float32 [4096], replicated, may hold values from 0.25 to 1.75
- gate_weight: bfloat16 [32, 4096, 192], P('ctx'), may hold values from -0.09375 to 0.09375
- up_weight: bfloat16 [32, 4096, 192], P('ctx'), may hold values from -0.09375 to 0.09375
- down_weight: bfloat16 [32, 192, 4096], P('ctx'), may hold values from -0.15625 to 0.15625
- routes: int32 [2, 4], P('group'), may hold values from 0 to 3, all different within a row; in each aligned block of 2 rows (0 to 1, 2 to 3, ...) at most 2 rows name the same one
- route_weight: float32 [2, 4], P('group'), may hold values from 0.1 to 1
Outputs:
- mixed: float32 [2, 4096], P('group', 'ctx')
Inputs may be any that keep to these rules, and one draw needn't show every extreme that they name: `routes`: each row names 4 different experts; no expert is named by more than 2 rows, a bound that some block reaches.
All inputs are finite; a program needn't handle non-finite values.
Results may differ from a plain program's by a relative error of at most 0.0035.
Values may be sent and summed in bfloat16 or wider, within the bound.
No kernel may reach another device: no remote copies, remote signals or barrier semaphores. Data moves between devices by JAX's collectives and lax.ppermute only.
A program may use at most 64 MiB of HBM per device.

v0:
```python
import jax
import jax.numpy as jnp
from jax import lax
from jax.sharding import PartitionSpec as P

QUARTERS = 8
eps = 1e-06


def slot_numbers(routes, expert_count):
    flat_routes = routes.reshape(-1)
    onehot = (flat_routes[:, None] == jnp.arange(expert_count, dtype=jnp.int32)[None, :]).astype(
        jnp.int32
    )
    before = jnp.cumsum(onehot, axis=0) - onehot
    return jnp.sum(before * onehot, axis=1)


def body(
    queries,
    key_cache,
    value_cache,
    out_weight,
    hidden_in,
    norm_gain,
    gate_weight,
    up_weight,
    down_weight,
    routes,
    route_weight,
):
    devices = lax.axis_size("ctx")
    my_index = lax.axis_index("ctx")
    seq_count, head_count, head_dim = queries.shape
    kv_heads = key_cache.shape[2] // head_dim
    group_size = head_count // kv_heads
    model_width = hidden_in.shape[1]
    local_len = key_cache.shape[1]
    query_view = queries.reshape(seq_count, kv_heads, group_size, head_dim)
    key_view = key_cache.reshape(seq_count, local_len, kv_heads, head_dim)
    value_view = value_cache.reshape(seq_count, local_len, kv_heads, head_dim)
    scores = jnp.einsum(
        "sgjd,scgd->sgjc", query_view, key_view, preferred_element_type=jnp.float32
    ) * head_dim ** (-0.5)
    row_peak = lax.pmax(jnp.max(scores, axis=-1), "ctx")
    numer = jnp.exp(scores - row_peak[..., None])
    denom_part = jnp.sum(numer, axis=-1)
    partial_value = jnp.einsum(
        "sgjc,scgd->sgjd",
        numer.astype(jnp.bfloat16),
        value_view,
        preferred_element_type=jnp.float32,
    )
    partial_value = partial_value.reshape(seq_count, head_count * head_dim)
    feat_dev = head_count * head_dim // devices
    feat_start = my_index * feat_dev
    summed, denoms = lax.psum((partial_value, denom_part), "ctx")
    attn_mine = lax.dynamic_slice_in_dim(summed, feat_start, feat_dev, 1)
    spread_denoms = jnp.repeat(denoms.reshape(seq_count, head_count), head_dim, axis=1)
    mine_denoms = lax.dynamic_slice_in_dim(spread_denoms, feat_start, feat_dev, 1)
    attended = (attn_mine / mine_denoms).astype(jnp.bfloat16)
    proj_part = jnp.dot(attended, out_weight, preferred_element_type=jnp.float32)
    col_dev = model_width // devices
    col_start = my_index * col_dev
    projected = lax.psum(proj_part, "ctx")
    resid = hidden_in.astype(jnp.float32) + projected
    inverse_rms = lax.rsqrt(jnp.mean(resid * resid, axis=-1, keepdims=True) + eps)
    normed = (resid * inverse_rms * norm_gain).astype(jnp.bfloat16)
    resid_mine = lax.dynamic_slice_in_dim(resid, col_start, col_dev, 1)
    expert_count = devices // QUARTERS
    top_count = routes.shape[1]
    capacity = min(2 * seq_count * top_count // expert_count, seq_count)
    expert = my_index // QUARTERS
    slot_index = slot_numbers(routes, expert_count)
    flat_routes = routes.reshape(-1)
    token_of = jnp.arange(seq_count * top_count, dtype=jnp.int32) // top_count
    matches = (
        (flat_routes[None, :] == expert)
        & (slot_index[None, :] == jnp.arange(capacity, dtype=jnp.int32)[:, None])
    ).astype(jnp.float32)
    owners = (token_of[:, None] == jnp.arange(seq_count, dtype=jnp.int32)[None, :]).astype(
        jnp.float32
    )
    select = jnp.dot(matches, owners, precision=lax.Precision.HIGHEST)
    slot_weight = jnp.dot(matches, route_weight.reshape(-1), precision=lax.Precision.HIGHEST)
    picked_rows = jnp.dot(
        select.astype(jnp.bfloat16), normed, preferred_element_type=jnp.float32
    ).astype(jnp.bfloat16)
    gate_act = jnp.dot(picked_rows, gate_weight[0], preferred_element_type=jnp.float32)
    up_act = jnp.dot(picked_rows, up_weight[0], preferred_element_type=jnp.float32)
    hidden = (jax.nn.silu(gate_act) * up_act).astype(jnp.bfloat16)
    expert_out = (
        jnp.dot(hidden, down_weight[0], preferred_element_type=jnp.float32) * slot_weight[:, None]
    )
    received = lax.all_to_all(
        expert_out.astype(jnp.bfloat16), "ctx", split_axis=1, concat_axis=0, tiled=True
    ).astype(expert_out.dtype)
    quarter_ids = jnp.arange(QUARTERS, dtype=jnp.int32)[None, None, :]
    shard_rows = (routes[:, :, None] * QUARTERS + quarter_ids) * capacity + slot_index.reshape(
        seq_count, top_count
    )[:, :, None]
    moe_mine = jnp.sum(received[shard_rows], axis=(1, 2))
    return resid_mine + moe_mine


def solution(mesh):
    in_specs = (
        P("group", None, None),
        P("group", "ctx", None),
        P("group", "ctx", None),
        P("ctx", None),
        P("group", None),
        P(),
        P("ctx", None, None),
        P("ctx", None, None),
        P("ctx", None, None),
        P("group", None),
        P("group", None),
    )
    out_specs = P("group", "ctx")
    return jax.shard_map(body, mesh=mesh, in_specs=in_specs, out_specs=out_specs, check_vma=False)
```

profile of v0, /device:TPU:0, one launch (start us, length us, event | category | flops | bytes accessed | tf_op | source)
XLA Modules:
  0.0 239.1 jit_solution(7500703949883063939)
XLA Ops:
  6.5 0.0 copy-start
  6.5 0.0 all-reduce.2.cloned.1.call-start
  6.5 1.4 fusion.41
  8.0 42.0 %pmax.7 = f32[2,4,16]{2,1,0:T(4,128)S(1)} all-reduce(f32[2,4,16]{2,1,0:T(4,128)S(1)} %get-tuple-element.7), channel_id=1, replica_groups=mesh['group'=1,'ctx'=32] {'ctx'}, use_global_device_ids=true, to_apply=%region_1.0 | all-reduce | flops 128 | bytes 1024 | tf_op jit(solution)/shard_map/pmax | solution.py:45
  50.0 0.0 copy-start.1
  50.0 0.0 copy-start.2
  50.0 1.2 fusion.17
  51.2 0.7 copy.38
  51.9 0.0 all-reduce.2.cloned.1.call-update
  51.9 0.8 broadcast_in_dim_reshape.2
  52.7 0.7 broadcast_multiply_fusion
  53.3 0.2 fusion.22
  53.6 0.8 reshape.100
  54.3 0.2 reduce_window_sum.11
  54.5 0.1 add.95
  54.6 0.1 reshape.87
  54.7 40.0 %psum.22 = f32[2,64]{1,0:T(2,128)S(1)} all-reduce(f32[2,64]{1,0:T(2,128)S(1)} %reshape.87), channel_id=1, replica_groups=mesh['group'=1,'ctx'=32] {'ctx'}, use_global_device_ids=true, to_apply=%region_4.0 | all-reduce | flops 128 | bytes 1024 | tf_op jit(solution)/shard_map/psum | solution.py:57
  94.7 0.1 broadcast_bitcast_fusion
  94.8 0.2 convolution_convert_fusion.1
  95.0 0.1 compare_select_fusion
  95.1 0.1 convolution_bitcast_fusion
  95.2 0.1 reshape.93
  95.3 0.1 copy.37
  95.3 76.0 %all-reduce.2.cloned.1.call-done = f32[2,8192]{1,0:T(2,128)} async-done(((f32[2,8192]{1,0:T(2,128)}), f32[2,8192]{1,0:T(2,128)}) %all-reduce.2.cloned.1.call-update) | async-done | bytes 65552 | tf_op jit(solution)/shard_map/psum | solution.py:57
  171.4 0.0 copy-done
  171.4 1.1 fusion.32
  172.4 41.0 %psum.23 = f32[2,4096]{1,0:T(2,128)S(1)} all-reduce(f32[2,4096]{1,0:T(2,128)S(1)} %fusion.32), channel_id=1, replica_groups=mesh['group'=1,'ctx'=32] {'ctx'}, use_global_device_ids=true, to_apply=%region_5.0 | all-reduce | flops 8192 | bytes 65536 | tf_op jit(solution)/shard_map/psum | solution.py:65
  213.4 0.0 copy-done.1
  213.5 0.1 multiply_reduce_fusion
  213.6 0.0 copy-done.2
  213.6 0.2 convolution_convert_fusion
  213.8 1.9 fusion.4
  215.8 3.7 %fusion.6 = bf16[2,32,128]{2,0,1:T(2,128)(2,1)} fusion(bf16[1,192,4096]{2,1,0:T(8,128)(2,1)} %param.19, bf16[2,4096]{1,0:T(2,128)(2,1)S(1)} %convolution_convert_fusion, bf16[1,4096,192]{1,2,0:T(8,128)(2,1)} %param.18, f32[2]{0:T(128)S(1)} %convolution_bitcast_fusion, f32[2,192]{1,0:T(2,128)S(1)} %fusion.4), kind=kOutput, calls=%fused_computation.10 | convolution fusion | flops 6310144 | bytes 3180040 | tf_op jit(solution)/shard_map/dot_general | solution.py:93
  219.5 4.4 %all-to-all-start = ((bf16[2,32,128]{2,0,1:T(2,128)(2,1)}), bf16[2,32,128]{2,0,1:T(2,128)(2,1)S(1)}, u32[]{:S(2)}, u32[]{:S(2)}) async-start(bf16[2,32,128]{2,0,1:T(2,128)(2,1)} %fusion.6), calls=%async_computation | async-start | bytes 32768 | tf_op jit(solution)/shard_map/all_to_all | solution.py:95
  223.9 7.2 %all-to-all-done = bf16[2,32,128]{2,0,1:T(2,128)(2,1)S(1)} async-done(((bf16[2,32,128]{2,0,1:T(2,128)(2,1)}), bf16[2,32,128]{2,0,1:T(2,128)(2,1)S(1)}, u32[]{:S(2)}, u32[]{:S(2)}) %all-to-all-start) | async-done | bytes 16416 | tf_op jit(solution)/shard_map/all_to_all | solution.py:95
  231.1 0.6 gather_fusion
  231.7 0.6 dynamic-slice_add_fusion
  (8 shorter events, 0.1 us)
Async XLA Ops:
  6.5 164.8 %copy-start = (bf16[256,4096]{1,0:T(8,128)(2,1)S(1)}, bf16[256,4096]{1,0:T(8,128)(2,1)}, u32[]{:S(2)}) copy-start(bf16[256,4096]{1,0:T(8,128)(2,1)} %param.14) | copy-start | bytes 6291460
  6.5 164.8 %all-reduce.2.cloned.1.call-start = ((), (), s32[]{:S(2)}) async-start(), calls=%async_computation.1 | async-start | bytes 131072 | tf_op jit(solution)/shard_map/psum | solution.py:57
  50.0 163.5 %copy-start.1 = (bf16[2,4096]{1,0:T(2,128)(2,1)S(1)}, bf16[2,4096]{1,0:T(2,128)(2,1)}, u32[]{:S(2)}) copy-start(bf16[2,4096]{1,0:T(2,128)(2,1)} %param.15) | copy-start | bytes 49156
  50.0 163.6 %copy-start.2 = (f32[4096]{0:T(1024)S(1)}, f32[4096]{0:T(1024)}, u32[]{:S(2)}) copy-start(f32[4096]{0:T(1024)} %param.16) | copy-start | bytes 49156
  219.5 11.6 %all-to-all-start = ((bf16[2,32,128]{2,0,1:T(2,128)(2,1)}), bf16[2,32,128]{2,0,1:T(2,128)(2,1)S(1)}, u32[]{:S(2)}, u32[]{:S(2)}) async-start(bf16[2,32,128]{2,0,1:T(2,128)(2,1)} %fusion.6), calls=%async_computation | async-start | bytes 32768 | tf_op jit(solution)/shard_map/all_to_all | solution.py:95
Sparse Core Ops, SparseCore 0:
  52.0 119.3 all-reduce.1
where the time goes:
time: 240 us; the launch traced here: 239 us
  blocking collectives  123 us (51%)
  waiting for transfers between devices  83.2 us (35%)
  between operations  13.5 us (6%)
  matrix products  9.84 us (4%)
  starting transfers between devices  4.4 us (2%)
  local copies, waits for them, and re-layouts  3.2 us (1%)
    psum x1, waiting for transfers between devices, body(): summed, denoms = lax.psum((partial_value, denom_part), 'ctx')  76 us
    pmax x1, blocking collectives, body(): row_peak = lax.pmax(jnp.max(scores, axis=-1), 'ctx')  42 us
    psum x1, blocking collectives, body(): projected = lax.psum(proj_part, 'ctx')  41 us
    psum x1, blocking collectives, body(): summed, denoms = lax.psum((partial_value, denom_part), 'ctx')  40 us
    all_to_all x1, waiting for transfers between devices, body(): lax.all_to_all(expert_out.astype(jnp.bfloat16), 'ctx', split_axis=1, conc...  7.16 us
  transfers between devices with their start and end apart: 2, of which 2 were waited for; matrix products, arithmetic and copies ran while one was open for 1% of the time, Pallas kernels for 0%

commit v1 on v0

--- a/solution.py
+++ b/solution.py
@@ -62,7 +62,7 @@
     proj_part = jnp.dot(attended, out_weight, preferred_element_type=jnp.float32)
     col_dev = model_width // devices
     col_start = my_index * col_dev
-    projected = lax.psum(proj_part, "ctx")
+    projected = jnp.sum(lax.all_gather(proj_part, "ctx"), axis=0)
     resid = hidden_in.astype(jnp.float32) + projected
     inverse_rms = lax.rsqrt(jnp.mean(resid * resid, axis=-1, keepdims=True) + eps)
     normed = (resid * inverse_rms * norm_gain).astype(jnp.bfloat16)

time: 240 us -> 256 us (1.067)
  waiting for transfers between devices: 83.2 us -> 141 us
  blocking collectives: 123 us -> 82.1 us
    all_gather x0 -> x1, waiting for transfers between devices: none -> 55 us  [body(): projected = jnp.sum(lax.all_gather(proj_part, 'ctx'), axis=0)]
    psum x1 -> x0, blocking collectives: 41 us -> none  [body(): projected = lax.psum(proj_part, 'ctx')]
    psum x1, waiting for transfers between devices: 76 us -> 78.8 us  [body(): summed, denoms = lax.psum((partial_value, denom_part), 'ctx')]
  transfers between devices with their start and end apart: 2 -> 3, of which waited for: 2 -> 3; matrix products, arithmetic and copies ran while one was open for 1% -> 1% of each run, Pallas kernels for 0% -> 0%
where the time goes in v1:
time: 256 us; the launch traced here: 255 us
  waiting for transfers between devices  141 us (55%)
  blocking collectives  82.1 us (32%)
  between operations  13.5 us (5%)
  matrix products  10.4 us (4%)
  starting transfers between devices  3.62 us (1%)
  other arithmetic  2.79 us (1%)
    psum x1, waiting for transfers between devices, body(): summed, denoms = lax.psum((partial_value, denom_part), 'ctx')  78.8 us
    all_gather x1, waiting for transfers between devices, body(): projected = jnp.sum(lax.all_gather(proj_part, 'ctx'), axis=0)  55 us
    pmax x1, blocking collectives, body(): row_peak = lax.pmax(jnp.max(scores, axis=-1), 'ctx')  42 us
    psum x1, blocking collectives, body(): summed, denoms = lax.psum((partial_value, denom_part), 'ctx')  40.1 us
    all_to_all x1, waiting for transfers between devices, body(): lax.all_to_all(expert_out.astype(jnp.bfloat16), 'ctx', split_axis=1, conc...  7.16 us
  transfers between devices with their start and end apart: 3, of which 3 were waited for; matrix products, arithmetic and copies ran while one was open for 1% of the time, Pallas kernels for 0%

profile of v1, /device:TPU:0, one launch (start us, length us, event | category | flops | bytes accessed | tf_op | source)
XLA Modules:
  0.0 255.4 jit_solution(15150535901822587929)
XLA Ops:
  6.5 0.0 copy-start
  6.5 0.0 all-reduce.2.cloned.1.call-start
  6.5 1.4 fusion.40
  8.0 0.0 copy-start.2
  8.0 0.0 copy-start.4
  8.0 42.0 %pmax.7 = f32[2,4,16]{2,1,0:T(4,128)S(1)} all-reduce(f32[2,4,16]{2,1,0:T(4,128)S(1)} %get-tuple-element.7), channel_id=1, replica_groups=mesh['group'=1,'ctx'=32] {'ctx'}, use_global_device_ids=true, to_apply=%region_1.0 | all-reduce | flops 128 | bytes 1024 | tf_op jit(solution)/shard_map/pmax | solution.py:45
  50.0 1.2 fusion.17
  51.2 0.7 copy.38
  51.9 0.0 all-reduce.2.cloned.1.call-update
  51.9 0.0 all-gather.4.cloned.1.call-start
  51.9 0.2 fusion.22
  52.1 0.1 reshape.87
  52.2 40.1 %psum.15 = f32[2,64]{1,0:T(2,128)S(1)} all-reduce(f32[2,64]{1,0:T(2,128)S(1)} %reshape.87), channel_id=1, replica_groups=mesh['group'=1,'ctx'=32] {'ctx'}, use_global_device_ids=true, to_apply=%region_4.0 | all-reduce | flops 128 | bytes 1024 | tf_op jit(solution)/shard_map/psum | solution.py:57
  92.3 0.1 broadcast_bitcast_fusion
  92.4 0.1 copy.37
  92.5 78.8 %all-reduce.2.cloned.1.call-done = f32[2,8192]{1,0:T(2,128)} async-done(((f32[2,8192]{1,0:T(2,128)}), f32[2,8192]{1,0:T(2,128)}) %all-reduce.2.cloned.1.call-update) | async-done | bytes 65552 | tf_op jit(solution)/shard_map/psum | solution.py:57
  171.3 0.0 copy-done
  171.3 0.0 copy-start.1
  171.3 0.0 copy-start.3
  171.3 1.7 convolution_bitcast_fusion
  173.0 0.0 all-gather.4.cloned.1.call-update
  173.0 0.0 copy-done.2
  173.0 0.1 broadcast_in_dim_reshape.2
  173.1 0.2 reduce_window_sum.11
  173.3 0.0 copy-done.4
  173.3 0.1 reshape.104
  173.4 0.1 add.93
  173.5 0.1 compare_select_fusion
  173.6 0.1 reshape.93
  173.7 0.1 convolution_bitcast_fusion.1
  173.8 0.2 convolution_convert_fusion.1
  174.0 55.0 %all-gather.4.cloned.1.call-done = f32[32,2,4096]{2,1,0:T(2,128)} async-done(((f32[1,2,4096]{2,1,0:T(2,128)}), f32[32,2,4096]{2,1,0:T(2,128)}) %all-gather.4.cloned.1.call-update) | async-done | bytes 1048592 | tf_op jit(solution)/shard_map/all_gather | solution.py:65
  229.0 1.5 reduce_sum.46
  230.6 0.0 copy-done.1
  230.6 0.1 multiply_reduce_fusion
  230.8 0.0 copy-done.3
  230.8 0.2 convolution_convert_fusion
  231.0 1.9 fusion.4
  232.9 3.7 %fusion.6 = bf16[2,32,128]{2,0,1:T(2,128)(2,1)} fusion(bf16[1,192,4096]{2,1,0:T(8,128)(2,1)} %param.19, bf16[2,4096]{1,0:T(2,128)(2,1)S(1)} %convolution_convert_fusion, bf16[1,4096,192]{1,2,0:T(8,128)(2,1)} %param.18, f32[2]{0:T(128)S(1)} %convolution_bitcast_fusion.1, f32[2,192]{1,0:T(2,128)S(1)} %fusion.4), kind=kOutput, calls=%fused_computation.11 | convolution fusion | flops 6310144 | bytes 3180040 | tf_op jit(solution)/shard_map/dot_general | solution.py:93
  236.6 3.6 %all-to-all-start = ((bf16[2,32,128]{2,0,1:T(2,128)(2,1)}), bf16[2,32,128]{2,0,1:T(2,128)(2,1)S(1)}, u32[]{:S(2)}, u32[]{:S(2)}) async-start(bf16[2,32,128]{2,0,1:T(2,128)(2,1)} %fusion.6), calls=%async_computation | async-start | bytes 32768 | tf_op jit(solution)/shard_map/all_to_all | solution.py:95
  240.2 7.2 %all-to-all-done = bf16[2,32,128]{2,0,1:T(2,128)(2,1)S(1)} async-done(((bf16[2,32,128]{2,0,1:T(2,128)(2,1)}), bf16[2,32,128]{2,0,1:T(2,128)(2,1)S(1)}, u32[]{:S(2)}, u32[]{:S(2)}) %all-to-all-start) | async-done | bytes 16416 | tf_op jit(solution)/shard_map/all_to_all | solution.py:95
  247.4 0.6 gather_fusion
  248.0 0.6 dynamic-slice_add_fusion
  (9 shorter events, 0.1 us)
Async XLA Ops:
  6.5 164.8 %copy-start = (bf16[256,4096]{1,0:T(8,128)(2,1)S(1)}, bf16[256,4096]{1,0:T(8,128)(2,1)}, u32[]{:S(2)}) copy-start(bf16[256,4096]{1,0:T(8,128)(2,1)} %param.14) | copy-start | bytes 6291460
  6.5 164.8 %all-reduce.2.cloned.1.call-start = ((), (), s32[]{:S(2)}) async-start(), calls=%async_computation.1 | async-start | bytes 131072 | tf_op jit(solution)/shard_map/psum | solution.py:57
  8.0 165.1 %copy-start.2 = (s32[2,4]{1,0:T(2,128)S(1)}, s32[2,4]{1,0:T(2,128)}, u32[]{:S(2)}) copy-start(s32[2,4]{1,0:T(2,128)} %param.20) | copy-start | bytes 100
  8.0 165.3 %copy-start.4 = (f32[2,4]{1,0:T(2,128)S(1)}, f32[2,4]{1,0:T(2,128)}, u32[]{:S(2)}) copy-start(f32[2,4]{1,0:T(2,128)} %param.21) | copy-start | bytes 100
  51.9 177.1 %all-gather.4.cloned.1.call-start = ((), (), s32[]{:S(2)}) async-start(), calls=%async_computation.2 | async-start | bytes 1081344 | tf_op jit(solution)/shard_map/all_gather | solution.py:65
  171.3 59.3 %copy-start.1 = (bf16[2,4096]{1,0:T(2,128)(2,1)S(1)}, bf16[2,4096]{1,0:T(2,128)(2,1)}, u32[]{:S(2)}) copy-start(bf16[2,4096]{1,0:T(2,128)(2,1)} %param.15) | copy-start | bytes 49156
  171.3 59.4 %copy-start.3 = (f32[4096]{0:T(1024)S(1)}, f32[4096]{0:T(1024)}, u32[]{:S(2)}) copy-start(f32[4096]{0:T(1024)} %param.16) | copy-start | bytes 49156
  236.6 10.8 %all-to-all-start = ((bf16[2,32,128]{2,0,1:T(2,128)(2,1)}), bf16[2,32,128]{2,0,1:T(2,128)(2,1)S(1)}, u32[]{:S(2)}, u32[]{:S(2)}) async-start(bf16[2,32,128]{2,0,1:T(2,128)(2,1)} %fusion.6), calls=%async_computation | async-start | bytes 32768 | tf_op jit(solution)/shard_map/all_to_all | solution.py:95
Sparse Core Ops, SparseCore 0:
  52.0 119.2 all-reduce.1
  174.2 54.8 all-gather.3
